TPU v7x, 256 devices: a whole 4x4x8 slice. The times are simulated.
256 devices in a mesh: dp: 8 (over z), expert: 32 (over x, y, core).
Axes of the slice: x: 4, y: 4, z: 8, core: 2. Of those that a mesh axis runs over, the one named last changes fastest.
Arguments:
- tokens: bfloat16 [65536, 2048], P(('dp', 'expert')), may hold values from -6 to 6
- expert_ranks: int32 [32, 65536], P(None, ('dp', 'expert')), may hold values from 0 to 65535, as said below
- capacity: int32 [32], replicated, may hold values from 512 to 1024, as said below
- weight_in: bfloat16 [32, 2048, 8192], P('expert', None, 'dp'), may hold values from -0.125 to 0.125
- weight_out: bfloat16 [32, 8192, 2048], P('expert', 'dp'), may hold values from -0.0625 to 0.0625
- gate_weights: float32 [32, 1024], P('expert', 'dp'), may hold values from 0.05 to 1
Outputs:
- combined: bfloat16 [65536, 2048], P(('dp', 'expert'))
Inputs may be any that keep to these rules, and one draw needn't show every extreme that they name: `expert_ranks`: for each expert the ranks are a permutation of 0 to 65535. Of the 256 tokens of one device, at most 8 have rank under 1024 for one expert; for an expert of capacity 1024, some devices have exactly 8. At least one expert has capacity 1024.
All inputs are finite; a program needn't handle non-finite values.
Results may differ from a plain program's by a relative error of at most 0.0053.
Values may be sent and summed in bfloat16 or wider, within the bound.
No kernel may reach another device: no remote copies, remote signals or barrier semaphores. Data moves between devices by JAX's collectives and lax.ppermute only.
A program may use at most 64 MiB of HBM per device.

v0:
```python
import jax
import jax.numpy as jnp
from jax import lax
from jax.sharding import Mesh
from jax.sharding import PartitionSpec as P

MOST = 8
LANES = 128
EXPERT = ("expert_0", "expert_1", "expert_2")
DP_EXPERT = ("dp", "expert_0", "expert_1", "expert_2")


def exclusive(values):
    return jnp.cumsum(values) - values


def on_device(tokens, expert_ranks, capacity, weight_in, weight_out, gate_weights):
    dp_count = lax.axis_size("dp")
    expert_count = lax.axis_size(EXPERT)
    token_count, width = tokens.shape
    slots_dp = gate_weights.shape[1]
    rows_all = expert_count * MOST
    own_dp = lax.axis_index("dp")
    own_expert = lax.axis_index(EXPERT)
    chosen = expert_ranks < capacity[:, None]
    chosen_int = chosen.astype(jnp.int32)
    counts = jnp.sum(chosen_int, axis=1)
    before = jnp.cumsum(chosen_int, axis=1) - chosen_int
    places = lax.broadcasted_iota(jnp.int32, (expert_count, MOST, token_count), 1)
    pack_table = jnp.logical_and(chosen[:, None, :], before[:, None, :] == places)
    pack_table = pack_table.astype(jnp.bfloat16).reshape(rows_all, token_count)
    packed = jnp.dot(pack_table, tokens, preferred_element_type=jnp.float32).astype(jnp.bfloat16)
    arrived_rows = lax.all_to_all(
        packed.reshape(expert_count, MOST, width), EXPERT, split_axis=0, concat_axis=0, tiled=True
    ).reshape(rows_all, width)
    device_ids = lax.broadcasted_iota(jnp.int32, (expert_count, expert_count), 0)
    expert_ids = lax.broadcasted_iota(jnp.int32, (expert_count, expert_count), 1)
    table = jnp.where(device_ids == own_expert, counts[None, :], 0)
    table = lax.psum(table.reshape(-1, LANES), EXPERT).reshape(expert_count, expert_count)
    arrived = jnp.sum(jnp.where(expert_ids == own_expert, table, 0), axis=1)
    plane_ids = lax.broadcasted_iota(jnp.int32, (dp_count, LANES), 0)
    lane_ids = lax.broadcasted_iota(jnp.int32, (dp_count, LANES), 1)
    plane_row = jnp.pad(jnp.sum(table, axis=0).astype(jnp.float32), (0, LANES - expert_count))
    both = jnp.concatenate(
        [
            jnp.where(plane_ids == own_dp, plane_row[None, :], 0.0),
            jnp.where(plane_ids == own_dp, gate_weights.reshape(-1, LANES), 0.0),
        ]
    )
    both = lax.psum(both, "dp")
    plane_counts = both[:dp_count].astype(jnp.int32)
    most_rows = jnp.max(plane_counts)
    earlier = jnp.logical_and(plane_ids < own_dp, lane_ids == own_expert)
    first_slot = jnp.sum(jnp.where(earlier, plane_counts, 0))
    gates_all = jnp.concatenate([both[dp_count:].reshape(-1), jnp.zeros((rows_all,), jnp.float32)])
    within = lax.broadcasted_iota(jnp.int32, (expert_count, MOST), 1)
    target = jnp.where(within < arrived[:, None], exclusive(arrived)[:, None] + within, -1).reshape(
        rows_all
    )

    def experts(rows, plane_rows):
        slot_ids = lax.broadcasted_iota(jnp.int32, (rows_all, plane_rows), 1)
        place_table = (target[:, None] == slot_ids).astype(jnp.bfloat16)
        plane = lax.dot_general(
            place_table, rows, (((0,), (0,)), ((), ())), preferred_element_type=jnp.float32
        ).astype(jnp.bfloat16)
        slot_rows = lax.all_gather(plane, "dp", axis=0, tiled=True)
        hidden = jnp.maximum(
            jnp.dot(slot_rows, weight_in[0], preferred_element_type=jnp.float32), 0.0
        ).astype(jnp.bfloat16)
        share = jnp.dot(hidden, weight_out[0], preferred_element_type=jnp.float32)
        out = lax.psum_scatter(
            share.astype(jnp.bfloat16), "dp", scatter_dimension=0, tiled=True
        ).astype(jnp.float32)
        gates = lax.dynamic_slice_in_dim(gates_all, first_slot, plane_rows, 0)
        scaled = (gates[:, None] * out).astype(jnp.bfloat16)
        returned = jnp.dot(place_table, scaled, preferred_element_type=jnp.float32)
        return returned.astype(jnp.bfloat16)

    fair = slots_dp + slots_dp // 4
    sent_back = lax.cond(
        most_rows <= fair,
        lambda rows: experts(rows, fair),
        lambda rows: experts(rows, rows_all),
        arrived_rows,
    )
    results = lax.all_to_all(
        sent_back.reshape(expert_count, MOST, width),
        EXPERT,
        split_axis=0,
        concat_axis=0,
        tiled=True,
    ).reshape(rows_all, width)
    combined = lax.dot_general(
        pack_table, results, (((0,), (0,)), ((), ())), preferred_element_type=jnp.float32
    )
    return combined.astype(jnp.bfloat16)


def solution(mesh):
    split = Mesh(
        mesh.devices.reshape(mesh.shape["dp"], 4, 4, 2), ("dp", "expert_0", "expert_1", "expert_2")
    )
    placed = (
        P(DP_EXPERT, None),
        P(None, DP_EXPERT),
        P(),
        P(EXPERT, None, "dp"),
        P(EXPERT, "dp", None),
        P(EXPERT, "dp"),
    )
    return jax.shard_map(
        on_device, mesh=split, in_specs=placed, out_specs=P(DP_EXPERT, None), check_vma=False
    )
```

profile of v0, /device:TPU:1, one launch (start us, length us, event | category | flops | bytes accessed | tf_op | source)
XLA Modules:
  0.0 348.8 jit_solution(17893966849262882347)
XLA Ops:
  6.5 0.0 copy-start
  6.5 0.0 copy-start.1
  6.5 0.9 convert_bitcast_fusion.1
  7.5 0.6 reduce-window.18
  8.1 0.2 slice_reduce_fusion
  8.3 0.1 iota.90
  8.4 0.1 convert_subtract_fusion
  8.5 0.0 copy-done
  8.5 1.5 fusion.19
  10.0 8.6 %all-to-all-start = ((bf16[32,8,2048]{2,1,0:T(8,128)(2,1)}), bf16[32,8,2048]{2,1,0:T(8,128)(2,1)S(1)}, u32[]{:S(2)}, u32[]{:S(2)}) async-start(bf16[32,8,2048]{2,1,0:T(8,128)(2,1)} %fusion.19), calls=%async_computation.2 | async-start | bytes 2097152 | tf_op jit(solution)/shard_map/all_to_all | solution.py:33
  18.6 0.1 iota.79
  18.7 0.1 iota.80
  18.8 0.1 broadcast_in_dim.57
  18.9 0.1 reshape.73
  18.9 127.0 %psum.14 = s32[32,32]{1,0:T(8,128)S(1)} all-reduce(s32[32,32]{1,0:T(8,128)S(1)} %reshape.73), channel_id=1, replica_groups=mesh['dp'=8,'expert_0'=4,'expert_1'=4,'expert_2'=2] {'expert_0','expert_..., use_global_device_ids=true, to_apply=%region_3.4 | all-reduce | flops 1024 | bytes 8192 | tf_op jit(solution)/shard_map/psum | solution.py:39
  145.9 0.1 select_reduce_fusion
  146.1 0.0 copy-done.1
  146.1 0.1 broadcast_select_fusion.1
  146.1 16.5 %psum.15 = f32[16,128]{1,0:T(8,128)S(1)} all-reduce(f32[16,128]{1,0:T(8,128)S(1)} %pad_maximum_fusion), channel_id=1, replica_groups=mesh['dp'=8,'expert_0'=4,'expert_1'=4,'expert_2'=2] {'dp'}, use_global_device_ids=true, to_apply=%region_5.6 | all-reduce | flops 2048 | bytes 16384 | tf_op jit(solution)/shard_map/psum | solution.py:50
  162.7 0.8 select_reduce_fusion.1
  164.2 0.1 copy.19
  164.2 0.1 reduce-window.20
  164.3 0.1 reduce.1
  164.4 0.1 add_select_fusion
  164.5 0.0 all-to-all-done
  164.5 151.7 %conditional.2 = (bf16[256,2048]{1,0:T(8,128)(2,1)S(1)}) conditional(s32[]{:T(128)} %convert_element_type.61, (s32[32,8]{1,0:T(8,128)S(1)}, s32[]{:T(128)}, f32[1280]{0:T(1024)S(1)}, bf16[256,2048]{1,0:T(8,128)(2,1)S(1)}, bf16[1,2048,1024]{2,1,0:T(8,128)(2,1)}, /*index=5*/bf16[1,1024,2048]{2,1,0:T(8,128)(2,1)}) %tuple.30, (s32[32,8]{1,0:T(8,128)S(1)}, ...), branch_computations={%region_10.12_spmd, %region_12.14_spmd} | conditional | flops 17727356928 | bytes 85990520
  164.5 0.0 all-gather.5.cloned.1.call-start
  164.6 0.1 eq.49
  164.7 1.3 convolution_convert_fusion.3
  166.0 0.0 all-gather.5.cloned.1.call-update
  166.0 0.2 reduce-scatter.5.cloned.1.call-start
  166.2 67.1 %all-gather.5.cloned.1.call-done = bf16[1280,2048]{1,0:T(8,128)(2,1)} async-done(((bf16[160,2048]{1,0:T(8,128)(2,1)}), bf16[1280,2048]{1,0:T(8,128)(2,1)}) %all-gather.5.cloned.1.call-update) | async-done | bytes 5242896 | tf_op jit(solution)/shard_map/cond/branch_1_fun/all_gather | solution.py:67
  233.4 16.9 %convolution_convert_fusion.2 = bf16[1280,2048]{1,0:T(8,128)(2,1)} fusion(bf16[1,1024,2048]{2,1,0:T(8,128)(2,1)} %get-tuple-element.45, bf16[1280,2048]{1,0:T(8,128)(2,1)} %all-gather.5.cloned.1.call-done, bf16[1,2048,1024]{2,1,0:T(8,128)(2,1)} %get-tuple-element.44), kind=kOutput, calls=%fused_computation.13 | convolution fusion | flops 10742661120 | bytes 18874368 | tf_op jit(solution)/shard_map/cond/branch_1_fun/dot_general | solution.py:71
  250.2 0.0 reduce-scatter.5.cloned.1.call-update
  252.0 0.1 dynamic_slice.5
  252.0 62.3 %reduce-scatter.5.cloned.1.call-done = bf16[160,2048]{1,0:T(8,128)(2,1)} async-done(((bf16[1280,2048]{1,0:T(8,128)(2,1)}), bf16[160,2048]{1,0:T(8,128)(2,1)}) %reduce-scatter.5.cloned.1.call-update) | async-done | bytes 655376 | tf_op jit(solution)/shard_map/cond/branch_1_fun/reduce_scatter | solution.py:72
  314.4 1.6 fusion.13
  316.2 24.3 %all_to_all.10 = bf16[32,8,2048]{2,1,0:T(8,128)(2,1)S(1)} all-to-all(bf16[32,8,2048]{2,1,0:T(8,128)(2,1)S(1)} %bitcast.57), channel_id=1, replica_groups=mesh['dp'=8,'expert_0'=4,'expert_1'=4,'expert_2'=2] {'expert_0','expert_..., dimensions={0} | all-to-all | bytes 2097152 | tf_op jit(solution)/shard_map/all_to_all | solution.py:87
  340.5 1.5 fusion.18
  (17 shorter events, 0.1 us)
Async XLA Ops:
  6.5 2.0 copy-start
  6.5 139.5 %copy-start.1 = (f32[1,128]{1,0:T(1,128)S(1)}, f32[1,128]{1,0:T(1,128)}, u32[]{:S(2)}) copy-start(f32[1,128]{1,0:T(1,128)} %param.13) | copy-start | bytes 1540
  10.0 154.5 %all-to-all-start = ((bf16[32,8,2048]{2,1,0:T(8,128)(2,1)}), bf16[32,8,2048]{2,1,0:T(8,128)(2,1)S(1)}, u32[]{:S(2)}, u32[]{:S(2)}) async-start(bf16[32,8,2048]{2,1,0:T(8,128)(2,1)} %fusion.19), calls=%async_computation.2 | async-start | bytes 2097152 | tf_op jit(solution)/shard_map/all_to_all | solution.py:33
  164.5 68.8 %all-gather.5.cloned.1.call-start = ((), (), s32[]{:S(2)}) async-start(), calls=%async_computation.6 | async-start | bytes 5898240 | tf_op jit(solution)/shard_map/cond/branch_1_fun/all_gather | solution.py:67
  166.0 148.4 %reduce-scatter.5.cloned.1.call-start = ((), (), s32[]{:S(2)}) async-start(), calls=%async_computation.7 | async-start | bytes 5898240 | tf_op jit(solution)/shard_map/cond/branch_1_fun/reduce_scatter | solution.py:72
Sparse Core Ops, SparseCore 0:
  167.1 66.1 all-gather.4
  250.4 63.9 reduce-scatter.4
where the time goes:
time: 349 us
  blocking collectives  168 us (48%)
  waiting for transfers between devices  129 us (37%)
  matrix products  22.7 us (7%)
  between operations  14.2 us (4%)
  starting transfers between devices  8.84 us (3%)
    psum x1, blocking collectives, on_device(): lax.psum(table.reshape(-1, LANES), EXPERT)  127 us
    all_gather x1, waiting for transfers between devices, experts(): slot_rows = lax.all_gather(plane, 'dp', axis=0, tiled=True)  67.1 us
    reduce_scatter x1, waiting for transfers between devices, experts(): lax.psum_scatter(share.astype(jnp.bfloat16), 'dp', scatter_dimension=0, t...  62.3 us
    all_to_all x1, blocking collectives, on_device(): lax.all_to_all(sent_back.reshape(expert_count, MOST, width), EXPERT, spli...  24.3 us
    dot_general x1, matrix products, experts(): share = jnp.dot(hidden, weight_out[0], preferred_element_type=jnp.float32)  16.9 us
    psum x1, blocking collectives, on_device(): both = lax.psum(both, 'dp')  16.5 us
    all_to_all x1, starting transfers between devices, on_device(): lax.all_to_all(packed.reshape(expert_count, MOST, width), EXPERT, split_a...  8.58 us
  transfers between devices with their start and end apart: 3, of which 2 were waited for; matrix products, arithmetic and copies ran while one was open for 1% of the time, Pallas kernels for 0%

commit v1 on v0

--- a/solution.py
+++ b/solution.py
@@ -36,7 +36,9 @@
     device_ids = lax.broadcasted_iota(jnp.int32, (expert_count, expert_count), 0)
     expert_ids = lax.broadcasted_iota(jnp.int32, (expert_count, expert_count), 1)
     table = jnp.where(device_ids == own_expert, counts[None, :], 0)
-    table = lax.psum(table.reshape(-1, LANES), EXPERT).reshape(expert_count, expert_count)
+    table = jnp.sum(lax.all_gather(table.reshape(-1, LANES), EXPERT), axis=0).reshape(
+        expert_count, expert_count
+    )
     arrived = jnp.sum(jnp.where(expert_ids == own_expert, table, 0), axis=1)
     plane_ids = lax.broadcasted_iota(jnp.int32, (dp_count, LANES), 0)
     lane_ids = lax.broadcasted_iota(jnp.int32, (dp_count, LANES), 1)

time: 349 us -> 251 us (0.72)
  blocking collectives: 168 us -> 73 us
    psum x1 -> x0, blocking collectives: 127 us -> none  [on_device(): lax.psum(table.reshape(-1, LANES), EXPERT)]
    all_gather x0 -> x1, blocking collectives: none -> 32.2 us  [on_device(): lax.all_gather(table.reshape(-1, LANES), EXPERT)]
where the time goes in v1:
time: 251 us
  waiting for transfers between devices  126 us (50%)
  blocking collectives  73 us (29%)
  matrix products  22.7 us (9%)
  between operations  14.2 us (6%)
  starting transfers between devices  8.84 us (4%)
  other arithmetic  2.99 us (1%)
    all_gather x1, waiting for transfers between devices, experts(): slot_rows = lax.all_gather(plane, 'dp', axis=0, tiled=True)  64.1 us
    reduce_scatter x1, waiting for transfers between devices, experts(): lax.psum_scatter(share.astype(jnp.bfloat16), 'dp', scatter_dimension=0, t...  62.3 us
    all_gather x1, blocking collectives, on_device(): lax.all_gather(table.reshape(-1, LANES), EXPERT)  32.2 us
    all_to_all x1, blocking collectives, on_device(): lax.all_to_all(sent_back.reshape(expert_count, MOST, width), EXPERT, spli...  24.3 us
    dot_general x1, matrix products, experts(): share = jnp.dot(hidden, weight_out[0], preferred_element_type=jnp.float32)  16.9 us
    psum x1, blocking collectives, on_device(): both = lax.psum(both, 'dp')  16.5 us
    all_to_all x1, starting transfers between devices, on_device(): lax.all_to_all(packed.reshape(expert_count, MOST, width), EXPERT, split_a...  8.58 us
  transfers between devices with their start and end apart: 3, of which 2 were waited for; matrix products, arithmetic and copies ran while one was open for 1% of the time, Pallas kernels for 0%

profile of v1, /device:TPU:1, one launch (start us, length us, event | category | flops | bytes accessed | tf_op | source)
XLA Modules:
  0.0 250.9 jit_solution(1714099159479907801)
XLA Ops:
  6.5 0.0 copy-start
  6.5 0.0 copy-start.1
  6.5 0.9 convert_bitcast_fusion.1
  7.5 0.6 reduce-window.18
  8.1 0.2 slice_reduce_fusion
  8.3 0.1 iota.90
  8.4 0.1 convert_subtract_fusion
  8.5 0.0 copy-done
  8.5 1.5 fusion.19
  10.0 8.6 %all-to-all-start = ((bf16[32,8,2048]{2,1,0:T(8,128)(2,1)}), bf16[32,8,2048]{2,1,0:T(8,128)(2,1)S(1)}, u32[]{:S(2)}, u32[]{:S(2)}) async-start(bf16[32,8,2048]{2,1,0:T(8,128)(2,1)} %fusion.19), calls=%async_computation.2 | async-start | bytes 2097152 | tf_op jit(solution)/shard_map/all_to_all | solution.py:33
  18.6 0.1 iota.79
  18.7 0.1 iota.80
  18.8 0.1 broadcast_in_dim.59
  18.9 32.2 %all_gather.9 = s32[32,8,128]{2,1,0:T(8,128)S(1)} all-gather(s32[1,8,128]{2,1,0:T(8,128)S(1)} %broadcast_select_fusion.2), channel_id=1, replica_groups=mesh['dp'=8,'expert_0'=4,'expert_1'=4,'expert_2'=2] {'expert_0','expert_..., dimensions={0}, use_global_device_ids=true | all-gather | bytes 135168 | tf_op jit(solution)/shard_map/all_gather | solution.py:39
  51.1 0.1 reshape.104
  51.2 0.1 select_reduce_fusion
  51.3 0.0 copy-done.1
  51.3 0.1 broadcast_select_fusion.1
  51.4 16.5 %psum.7 = f32[16,128]{1,0:T(8,128)S(1)} all-reduce(f32[16,128]{1,0:T(8,128)S(1)} %pad_maximum_fusion), channel_id=1, replica_groups=mesh['dp'=8,'expert_0'=4,'expert_1'=4,'expert_2'=2] {'dp'}, use_global_device_ids=true, to_apply=%region_5.6 | all-reduce | flops 2048 | bytes 16384 | tf_op jit(solution)/shard_map/psum | solution.py:52
  67.9 0.8 select_reduce_fusion.1
  69.4 0.1 copy.19
  69.5 0.1 reduce-window.20
  69.5 0.1 reduce.1
  69.7 0.1 add_select_fusion
  69.8 0.0 all-to-all-done
  69.8 148.6 %conditional.2 = (bf16[256,2048]{1,0:T(8,128)(2,1)S(1)}) conditional(s32[]{:T(128)} %convert_element_type.61, (s32[32,8]{1,0:T(8,128)S(1)}, s32[]{:T(128)}, f32[1280]{0:T(1024)S(1)}, bf16[256,2048]{1,0:T(8,128)(2,1)S(1)}, bf16[1,2048,1024]{2,1,0:T(8,128)(2,1)}, /*index=5*/bf16[1,1024,2048]{2,1,0:T(8,128)(2,1)}) %tuple.30, (s32[32,8]{1,0:T(8,128)S(1)}, ...), branch_computations={%region_10.12_spmd, %region_12.14_spmd} | conditional | flops 17727356928 | bytes 85990520
  69.8 0.0 all-gather.5.cloned.1.call-start
  69.8 0.1 eq.49
  69.9 1.3 convolution_convert_fusion.3
  71.2 0.0 all-gather.5.cloned.1.call-update
  71.3 0.2 reduce-scatter.5.cloned.1.call-start
  71.5 64.1 %all-gather.5.cloned.1.call-done = bf16[1280,2048]{1,0:T(8,128)(2,1)} async-done(((bf16[160,2048]{1,0:T(8,128)(2,1)}), bf16[1280,2048]{1,0:T(8,128)(2,1)}) %all-gather.5.cloned.1.call-update) | async-done | bytes 5242896 | tf_op jit(solution)/shard_map/cond/branch_1_fun/all_gather | solution.py:69
  135.5 16.9 %convolution_convert_fusion.2 = bf16[1280,2048]{1,0:T(8,128)(2,1)} fusion(bf16[1,1024,2048]{2,1,0:T(8,128)(2,1)} %get-tuple-element.45, bf16[1280,2048]{1,0:T(8,128)(2,1)} %all-gather.5.cloned.1.call-done, bf16[1,2048,1024]{2,1,0:T(8,128)(2,1)} %get-tuple-element.44), kind=kOutput, calls=%fused_computation.13 | convolution fusion | flops 10742661120 | bytes 18874368 | tf_op jit(solution)/shard_map/cond/branch_1_fun/dot_general | solution.py:73
  152.4 0.0 reduce-scatter.5.cloned.1.call-update
  154.1 0.1 dynamic_slice.5
  154.2 62.3 %reduce-scatter.5.cloned.1.call-done = bf16[160,2048]{1,0:T(8,128)(2,1)} async-done(((bf16[1280,2048]{1,0:T(8,128)(2,1)}), bf16[160,2048]{1,0:T(8,128)(2,1)}) %reduce-scatter.5.cloned.1.call-update) | async-done | bytes 655376 | tf_op jit(solution)/shard_map/cond/branch_1_fun/reduce_scatter | solution.py:74
  216.5 1.6 fusion.13
  218.4 24.3 %all_to_all.10 = bf16[32,8,2048]{2,1,0:T(8,128)(2,1)S(1)} all-to-all(bf16[32,8,2048]{2,1,0:T(8,128)(2,1)S(1)} %bitcast.57), channel_id=1, replica_groups=mesh['dp'=8,'expert_0'=4,'expert_1'=4,'expert_2'=2] {'expert_0','expert_..., dimensions={0} | all-to-all | bytes 2097152 | tf_op jit(solution)/shard_map/all_to_all | solution.py:89
  242.6 1.5 fusion.18
  (18 shorter events, 0.2 us)
Async XLA Ops:
  6.5 2.0 copy-start
  6.5 44.8 %copy-start.1 = (f32[1,128]{1,0:T(1,128)S(1)}, f32[1,128]{1,0:T(1,128)}, u32[]{:S(2)}) copy-start(f32[1,128]{1,0:T(1,128)} %param.13) | copy-start | bytes 1540
  10.0 59.8 %all-to-all-start = ((bf16[32,8,2048]{2,1,0:T(8,128)(2,1)}), bf16[32,8,2048]{2,1,0:T(8,128)(2,1)S(1)}, u32[]{:S(2)}, u32[]{:S(2)}) async-start(bf16[32,8,2048]{2,1,0:T(8,128)(2,1)} %fusion.19), calls=%async_computation.2 | async-start | bytes 2097152 | tf_op jit(solution)/shard_map/all_to_all | solution.py:33
  69.8 65.7 %all-gather.5.cloned.1.call-start = ((), (), s32[]{:S(2)}) async-start(), calls=%async_computation.6 | async-start | bytes 5898240 | tf_op jit(solution)/shard_map/cond/branch_1_fun/all_gather | solution.py:69
  71.3 145.3 %reduce-scatter.5.cloned.1.call-start = ((), (), s32[]{:S(2)}) async-start(), calls=%async_computation.7 | async-start | bytes 5898240 | tf_op jit(solution)/shard_map/cond/branch_1_fun/reduce_scatter | solution.py:74
Sparse Core Ops, SparseCore 0:
  72.4 63.1 all-gather.4
  152.6 63.9 reduce-scatter.4
